TPU v7x, 512 devices: a whole 4x8x8 slice. The times are simulated.
512 devices in a mesh: grid: 32 (over y, x), band: 16 (over z, core).
Axes of the slice: x: 4, y: 8, z: 8, core: 2. Of those that a mesh axis runs over, the one named last changes fastest.
Arguments:
- start: float32 [1, 4, 1, 64, 32768], P(None, None, None, 'band', 'grid'), may hold values from -6 to 6
- energies: float32 [4, 64, 32768], P(None, 'band', 'grid'), may hold values from -4 to 4
- sites: int32 [3, 1], replicated, may hold values from 0 to 31
- potential: float32 [32, 32, 32], replicated, may hold values from -4 to 400
Outputs:
- alphas: float32 [1, 1, 4], replicated
- betas: float32 [1, 1, 4], replicated
- lanczos: float32 [1, 4, 1, 64, 32768], P(None, None, None, 'band', 'grid')
All inputs are finite; a program needn't handle non-finite values.
Results may differ from a plain program's by a relative error of at most 0.0003.
Values sent between devices are 32-bit elements; how exact they have to be, the bound alone decides.
A program may use at most 64 MiB of HBM per device.

v0:
```python
import functools
import math
import jax
import jax.numpy as jnp
from jax import lax
from jax.sharding import Mesh
from jax.sharding import PartitionSpec as P

ITERS = 4
GRID = ("grid_0", "grid_1")
BAND = ("band_0", "band_1")
GRID_BAND = ("grid_0", "grid_1", "band_0", "band_1")
precise_mode = lax.Precision.HIGHEST


def one_axis_at_a_time(x, axes):
    return functools.reduce(lax.psum, axes, x)


def cas_table(grid_size):
    cells = jnp.arange(grid_size, dtype=jnp.int32)
    phase = cells[:, None] * cells[None, :] % grid_size
    angle = phase.astype(jnp.float32) * (2.0 * math.pi / grid_size)
    return jnp.cos(angle) + jnp.sin(angle)


def shift_axis(field_part, offset, axis_number):
    length = field_part.shape[axis_number]
    doubled = jnp.concatenate([field_part, field_part], axis=axis_number)
    first_index = (length - offset) % length
    return lax.dynamic_slice_in_dim(doubled, first_index, length, axis_number)


def expand_coef(values):
    return values[:, None, :, None, None]


def body(start, energies, sites, potential):
    grid_size = potential.shape[0]
    volume = grid_size * grid_size * grid_size
    atom_count, core_count, pol_count, band_local, kpoint_local = start.shape
    plane_count = grid_size // lax.axis_size(GRID)
    position = lax.axis_index(GRID)
    chain_count = core_count * pol_count * band_local
    field_count = atom_count * chain_count
    total_count = core_count * band_local * lax.axis_size(BAND) * kpoint_local * lax.axis_size(GRID)
    cas_grid = cas_table(grid_size)
    shifted = shift_axis(potential, sites[0, 0], 0)
    shifted = shift_axis(shifted, sites[1, 0], 1)
    shifted = shift_axis(shifted, sites[2, 0], 2)
    tables = [shifted]
    shifted_all = jnp.stack(tables, axis=-1)
    slab_table = lax.dynamic_slice_in_dim(shifted_all, position * plane_count, plane_count, 1)

    def moment(left, right):
        return jnp.sum(left * right, axis=(1, 3, 4)) / total_count

    start_sum = one_axis_at_a_time(moment(start, start), GRID_BAND)
    lanczos = start / expand_coef(jnp.sqrt(start_sum))
    previous = jnp.zeros_like(start)
    beta_prev = jnp.zeros((atom_count, pol_count), jnp.float32)
    alpha_list = []
    beta_list = []
    for iteration in range(ITERS):
        spread_fields = lanczos.reshape(atom_count, chain_count, plane_count, grid_size, grid_size)
        spread_over_z = jnp.einsum(
            "arpyz,wz->pywar", spread_fields, cas_grid, precision=precise_mode
        )
        spread_over_y = jnp.einsum(
            "pywar,uy->puwar", spread_over_z, cas_grid, precision=precise_mode
        )
        direct_spectrum = lax.all_to_all(
            spread_over_y.reshape(plane_count, grid_size, grid_size, field_count),
            GRID,
            split_axis=1,
            concat_axis=0,
            tiled=True,
        )
        field_shape = direct_spectrum.shape
        over_x = jnp.einsum("xvwf,tx->tvwf", direct_spectrum, cas_grid, precision=precise_mode)
        split_view = over_x.reshape(
            field_shape[0], field_shape[1], field_shape[2], atom_count, chain_count
        )
        scaled = split_view * slab_table[..., None]
        back_x = jnp.einsum("tvwar,xt->xvwar", scaled, cas_grid, precision=precise_mode)
        weighted = back_x.reshape(field_shape)
        direct_returned = lax.all_to_all(weighted, GRID, split_axis=0, concat_axis=1, tiled=True)
        fields = direct_returned.reshape(plane_count, grid_size, grid_size, atom_count, chain_count)
        over_z = jnp.einsum("pvwar,zw->pvzar", fields, cas_grid, precision=precise_mode)
        over_y = jnp.einsum("pvzar,yv->arpyz", over_z, cas_grid, precision=precise_mode)
        applied = energies[None, :, None] * lanczos - over_y.reshape(start.shape) / volume
        moments_all = (
            one_axis_at_a_time(moment(lanczos, applied), GRID_BAND),
            one_axis_at_a_time(moment(applied, applied), GRID_BAND),
            one_axis_at_a_time(moment(lanczos, lanczos), GRID_BAND),
            one_axis_at_a_time(moment(previous, previous), GRID_BAND),
            one_axis_at_a_time(moment(previous, applied), GRID_BAND),
            one_axis_at_a_time(moment(lanczos, previous), GRID_BAND),
        )
        alpha_now = moments_all[0]
        square = (
            moments_all[1]
            + alpha_now * alpha_now * moments_all[2]
            + beta_prev * beta_prev * moments_all[3]
        )
        square = square - 2.0 * alpha_now * moments_all[0] - 2.0 * beta_prev * moments_all[4]
        square = square + 2.0 * alpha_now * beta_prev * moments_all[5]
        beta_now = jnp.sqrt(square)
        remainder = applied - expand_coef(alpha_now) * lanczos - expand_coef(beta_prev) * previous
        previous = lanczos
        lanczos = remainder / expand_coef(beta_now)
        beta_prev = beta_now
        alpha_list.append(alpha_now)
        beta_list.append(beta_now)
    return (jnp.stack(alpha_list, axis=2), jnp.stack(beta_list, axis=2), lanczos)


def solution(mesh):
    split = Mesh(mesh.devices.reshape(8, 4, 8, 2), ("grid_0", "grid_1", "band_0", "band_1"))
    placed = (P(None, None, None, BAND, GRID), P(None, BAND, GRID), P(), P())
    return jax.shard_map(
        body,
        mesh=split,
        in_specs=placed,
        out_specs=(P(), P(), P(None, None, None, BAND, GRID)),
        check_vma=False,
    )
```

profile of v0, /device:TPU:1, one launch (start us, length us, event | category | flops | bytes accessed | tf_op | source)
XLA Modules:
  0.0 446.5 jit_solution(14919644235281792380)
XLA Ops:
  0.6 1.5 multiply_reduce_fusion.20
  2.8 15.8 %psum.652 = f32[1,1]{1,0:T(1,128)} all-reduce(f32[1,1]{1,0:T(1,128)} %bitcast), channel_id=1, replica_groups=mesh['grid_0'=8,'grid_1'=4,'band_0'=8,'band_1'=2] {'grid_0'}, use_global_device_ids=true, to_apply=%region_1.2 | all-reduce | flops 1 | bytes 8 | tf_op jit(solution)/shard_map/psum | solution.py:17
  18.6 9.1 %psum.653 = f32[1,1]{1,0:T(1,128)} all-reduce(f32[1,1]{1,0:T(1,128)} %psum.652), channel_id=1, replica_groups=mesh['grid_0'=8,'grid_1'=4,'band_0'=8,'band_1'=2] {'grid_1'}, use_global_device_ids=true, to_apply=%region_2.3 | all-reduce | flops 1 | bytes 8 | tf_op jit(solution)/shard_map/psum | solution.py:17
  27.7 20.0 %psum.654 = f32[1,1]{1,0:T(1,128)} all-reduce(f32[1,1]{1,0:T(1,128)} %psum.653), channel_id=1, replica_groups=mesh['grid_0'=8,'grid_1'=4,'band_0'=8,'band_1'=2] {'band_0'}, use_global_device_ids=true, to_apply=%region_3.4 | all-reduce | flops 1 | bytes 8 | tf_op jit(solution)/shard_map/psum | solution.py:17
  47.8 12.9 %psum.655 = f32[1,1]{1,0:T(1,128)} all-reduce(f32[1,1]{1,0:T(1,128)} %psum.654), channel_id=1, replica_groups=mesh['grid_0'=8,'grid_1'=4,'band_0'=8,'band_1'=2] {'band_1'}, use_global_device_ids=true, to_apply=%region_4.5 | all-reduce | flops 1 | bytes 8 | tf_op jit(solution)/shard_map/psum | solution.py:17
  62.9 1.3 convolution_bitcast_fusion.14
  65.2 4.8 %all-to-all-start = ((f32[32,1,512]{2,1,0:T(1,128)}), f32[32,1,512]{2,1,0:T(1,128)S(1)}, u32[]{:S(2)}, u32[]{:S(2)}) async-start(f32[32,1,512]{2,1,0:T(1,128)} %reshape.373), calls=%async_computation | async-start | bytes 131072 | tf_op jit(solution)/shard_map/all_to_all | solution.py:72
  73.2 5.6 %all-to-all-done = f32[32,1,512]{2,1,0:T(1,128)S(1)} async-done(((f32[32,1,512]{2,1,0:T(1,128)}), f32[32,1,512]{2,1,0:T(1,128)S(1)}, u32[]{:S(2)}, u32[]{:S(2)}) %all-to-all-start) | async-done | bytes 65568 | tf_op jit(solution)/shard_map/all_to_all | solution.py:72
  81.6 12.2 %all_to_all.32 = f32[32,1,512]{2,1,0:T(1,128)S(1)} all-to-all(f32[32,1,512]{2,1,0:T(1,128)S(1)} %reshape.375), channel_id=1, replica_groups=mesh['grid_0'=8,'grid_1'=4,'band_0'=8,'band_1'=2] {'grid_0','grid_1'}, dimensions={0} | all-to-all | bytes 131072 | tf_op jit(solution)/shard_map/all_to_all | solution.py:87
  94.7 1.3 convolution_bitcast_fusion.12
  96.0 1.3 fusion.3
  102.0 15.3 %all-reduce.7 = (f32[1,1]{1,0:T(1,128)}, f32[1,1]{1,0:T(1,128)}, f32[1,1]{1,0:T(1,128)}, f32[1,1]{1,0:T(1,128)}, f32[1,1]{1,0:T(1,128)}, /*index=5*/f32[1,1]{1,0:T(1,128)}) all-reduce(f32[1,1]{1,0:T(1,128)} %bitcast.24, f32[1,1]{1,0:T(1,128)} %bitcast.21, ...), channel_id=1, replica_groups=mesh['grid_0'=8,'grid_1'=4,'band_0'=8,'band_1'=2] {'grid_0'}, use_global_device_ids=true, to_apply=%region_11.12 | all-reduce | flops 6 | bytes 48 | tf_op jit(solution)/shard_map/psum | solution.py:17
  117.3 7.8 %all-reduce.11 = (f32[1,1]{1,0:T(1,128)}, f32[1,1]{1,0:T(1,128)}, f32[1,1]{1,0:T(1,128)}, f32[1,1]{1,0:T(1,128)}, f32[1,1]{1,0:T(1,128)}, /*index=5*/f32[1,1]{1,0:T(1,128)}) all-reduce(f32[1,1]{1,0:T(1,128)} %get-tuple-element.59, ...), channel_id=1, replica_groups=mesh['grid_0'=8,'grid_1'=4,'band_0'=8,'band_1'=2] {'grid_1'}, use_global_device_ids=true, to_apply=%region_12.13 | all-reduce | flops 6 | bytes 48 | tf_op jit(solution)/shard_map/psum | solution.py:17
  125.0 11.4 %all-reduce.3 = (f32[1,1]{1,0:T(1,128)}, f32[1,1]{1,0:T(1,128)}, f32[1,1]{1,0:T(1,128)}, f32[1,1]{1,0:T(1,128)}, f32[1,1]{1,0:T(1,128)}, /*index=5*/f32[1,1]{1,0:T(1,128)}) all-reduce(f32[1,1]{1,0:T(1,128)} %get-tuple-element.80, ...), channel_id=1, replica_groups=mesh['grid_0'=8,'grid_1'=4,'band_0'=8,'band_1'=2] {'band_0'}, use_global_device_ids=true, to_apply=%region_13.14 | all-reduce | flops 6 | bytes 48 | tf_op jit(solution)/shard_map/psum | solution.py:17
  136.4 14.4 %all-reduce.15 = (f32[1,1]{1,0:T(1,128)}, f32[1,1]{1,0:T(1,128)}, f32[1,1]{1,0:T(1,128)}, f32[1,1]{1,0:T(1,128)}, f32[1,1]{1,0:T(1,128)}, /*index=5*/f32[1,1]{1,0:T(1,128)}) all-reduce(f32[1,1]{1,0:T(1,128)} %get-tuple-element.38, ...), channel_id=1, replica_groups=mesh['grid_0'=8,'grid_1'=4,'band_0'=8,'band_1'=2] {'band_1'}, use_global_device_ids=true, to_apply=%region_14.15 | all-reduce | flops 6 | bytes 48 | tf_op jit(solution)/shard_map/psum | solution.py:17
  158.3 1.3 convolution_bitcast_fusion.11
  159.6 1.3 convolution_bitcast_fusion.10
  161.2 13.1 %all_to_all.33 = f32[32,1,512]{2,1,0:T(1,128)S(1)} all-to-all(f32[32,1,512]{2,1,0:T(1,128)S(1)} %reshape.377), channel_id=1, replica_groups=mesh['grid_0'=8,'grid_1'=4,'band_0'=8,'band_1'=2] {'grid_0','grid_1'}, dimensions={0} | all-to-all | bytes 131072 | tf_op jit(solution)/shard_map/all_to_all | solution.py:72
  177.1 4.0 all-to-all-start.3
  181.8 8.2 %all-to-all-done.3 = f32[32,1,512]{2,1,0:T(1,128)S(1)} async-done(((f32[32,1,512]{2,1,0:T(1,128)}), f32[32,1,512]{2,1,0:T(1,128)S(1)}, u32[]{:S(2)}, u32[]{:S(2)}) %all-to-all-start.3) | async-done | bytes 65568 | tf_op jit(solution)/shard_map/all_to_all | solution.py:87
  190.9 1.3 convolution_bitcast_fusion.8
  192.2 1.3 fusion.2
  197.5 14.6 %all-reduce.6 = (f32[1,1]{1,0:T(1,128)}, f32[1,1]{1,0:T(1,128)}, f32[1,1]{1,0:T(1,128)}, f32[1,1]{1,0:T(1,128)}, f32[1,1]{1,0:T(1,128)}) all-reduce(f32[1,1]{1,0:T(1,128)} %bitcast.45, f32[1,1]{1,0:T(1,128)} %bitcast.42, f32[1,1]{1,0:T(1,128)} %bitcast.46, ...), channel_id=1, replica_groups=mesh['grid_0'=8,'grid_1'=4,'band_0'=8,'band_1'=2] {'grid_0'}, use_global_device_ids=true, to_apply=%region_40.41 | all-reduce | flops 5 | bytes 40 | tf_op jit(solution)/shard_map/psum | solution.py:17
  212.2 7.5 %all-reduce.10 = (f32[1,1]{1,0:T(1,128)}, f32[1,1]{1,0:T(1,128)}, f32[1,1]{1,0:T(1,128)}, f32[1,1]{1,0:T(1,128)}, f32[1,1]{1,0:T(1,128)}) all-reduce(f32[1,1]{1,0:T(1,128)} %get-tuple-element.54, f32[1,1]{1,0:T(1,128)} %get-tuple-element.55, ...), channel_id=1, replica_groups=mesh['grid_0'=8,'grid_1'=4,'band_0'=8,'band_1'=2] {'grid_1'}, use_global_device_ids=true, to_apply=%region_41.42 | all-reduce | flops 5 | bytes 40 | tf_op jit(solution)/shard_map/psum | solution.py:17
  219.7 13.1 %all-reduce.2 = (f32[1,1]{1,0:T(1,128)}, f32[1,1]{1,0:T(1,128)}, f32[1,1]{1,0:T(1,128)}, f32[1,1]{1,0:T(1,128)}, f32[1,1]{1,0:T(1,128)}) all-reduce(f32[1,1]{1,0:T(1,128)} %get-tuple-element.75, f32[1,1]{1,0:T(1,128)} %get-tuple-element.76, ...), channel_id=1, replica_groups=mesh['grid_0'=8,'grid_1'=4,'band_0'=8,'band_1'=2] {'band_0'}, use_global_device_ids=true, to_apply=%region_42.43 | all-reduce | flops 5 | bytes 40 | tf_op jit(solution)/shard_map/psum | solution.py:17
  232.8 15.3 %all-reduce.14 = (f32[1,1]{1,0:T(1,128)}, f32[1,1]{1,0:T(1,128)}, f32[1,1]{1,0:T(1,128)}, f32[1,1]{1,0:T(1,128)}, f32[1,1]{1,0:T(1,128)}) all-reduce(f32[1,1]{1,0:T(1,128)} %get-tuple-element.33, f32[1,1]{1,0:T(1,128)} %get-tuple-element.34, ...), channel_id=1, replica_groups=mesh['grid_0'=8,'grid_1'=4,'band_0'=8,'band_1'=2] {'band_1'}, use_global_device_ids=true, to_apply=%region_43.44 | all-reduce | flops 5 | bytes 40 | tf_op jit(solution)/shard_map/psum | solution.py:17
  255.3 1.3 convolution_bitcast_fusion.6
  256.9 13.0 %all_to_all.34 = f32[32,1,512]{2,1,0:T(1,128)S(1)} all-to-all(f32[32,1,512]{2,1,0:T(1,128)S(1)} %reshape.381), channel_id=1, replica_groups=mesh['grid_0'=8,'grid_1'=4,'band_0'=8,'band_1'=2] {'grid_0','grid_1'}, dimensions={0} | all-to-all | bytes 131072 | tf_op jit(solution)/shard_map/all_to_all | solution.py:72
  272.8 3.9 all-to-all-start.5
  277.3 8.3 %all-to-all-done.5 = f32[32,1,512]{2,1,0:T(1,128)S(1)} async-done(((f32[32,1,512]{2,1,0:T(1,128)}), f32[32,1,512]{2,1,0:T(1,128)S(1)}, u32[]{:S(2)}, u32[]{:S(2)}) %all-to-all-start.5) | async-done | bytes 65568 | tf_op jit(solution)/shard_map/all_to_all | solution.py:87
  286.5 1.3 convolution_bitcast_fusion.4
  287.9 1.3 fusion.1
  293.3 14.6 %all-reduce.5 = (f32[1,1]{1,0:T(1,128)}, f32[1,1]{1,0:T(1,128)}, f32[1,1]{1,0:T(1,128)}, f32[1,1]{1,0:T(1,128)}, f32[1,1]{1,0:T(1,128)}) all-reduce(f32[1,1]{1,0:T(1,128)} %bitcast.66, f32[1,1]{1,0:T(1,128)} %bitcast.63, f32[1,1]{1,0:T(1,128)} %bitcast.67, ...), channel_id=1, replica_groups=mesh['grid_0'=8,'grid_1'=4,'band_0'=8,'band_1'=2] {'grid_0'}, use_global_device_ids=true, to_apply=%region_65.66 | all-reduce | flops 5 | bytes 40 | tf_op jit(solution)/shard_map/psum | solution.py:17
  307.9 7.5 %all-reduce.9 = (f32[1,1]{1,0:T(1,128)}, f32[1,1]{1,0:T(1,128)}, f32[1,1]{1,0:T(1,128)}, f32[1,1]{1,0:T(1,128)}, f32[1,1]{1,0:T(1,128)}) all-reduce(f32[1,1]{1,0:T(1,128)} %get-tuple-element.49, f32[1,1]{1,0:T(1,128)} %get-tuple-element.50, ...), channel_id=1, replica_groups=mesh['grid_0'=8,'grid_1'=4,'band_0'=8,'band_1'=2] {'grid_1'}, use_global_device_ids=true, to_apply=%region_66.67 | all-reduce | flops 5 | bytes 40 | tf_op jit(solution)/shard_map/psum | solution.py:17
  315.4 11.4 %all-reduce.1 = (f32[1,1]{1,0:T(1,128)}, f32[1,1]{1,0:T(1,128)}, f32[1,1]{1,0:T(1,128)}, f32[1,1]{1,0:T(1,128)}, f32[1,1]{1,0:T(1,128)}) all-reduce(f32[1,1]{1,0:T(1,128)} %get-tuple-element.70, f32[1,1]{1,0:T(1,128)} %get-tuple-element.71, ...), channel_id=1, replica_groups=mesh['grid_0'=8,'grid_1'=4,'band_0'=8,'band_1'=2] {'band_0'}, use_global_device_ids=true, to_apply=%region_67.68 | all-reduce | flops 5 | bytes 40 | tf_op jit(solution)/shard_map/psum | solution.py:17
  326.8 15.0 %all-reduce.13 = (f32[1,1]{1,0:T(1,128)}, f32[1,1]{1,0:T(1,128)}, f32[1,1]{1,0:T(1,128)}, f32[1,1]{1,0:T(1,128)}, f32[1,1]{1,0:T(1,128)}) all-reduce(f32[1,1]{1,0:T(1,128)} %get-tuple-element.28, f32[1,1]{1,0:T(1,128)} %get-tuple-element.29, ...), channel_id=1, replica_groups=mesh['grid_0'=8,'grid_1'=4,'band_0'=8,'band_1'=2] {'band_1'}, use_global_device_ids=true, to_apply=%region_68.69 | all-reduce | flops 5 | bytes 40 | tf_op jit(solution)/shard_map/psum | solution.py:17
  347.5 1.3 convolution_bitcast_fusion.3
  348.8 1.3 convolution_bitcast_fusion.2
  350.5 13.0 %all_to_all.35 = f32[32,1,512]{2,1,0:T(1,128)S(1)} all-to-all(f32[32,1,512]{2,1,0:T(1,128)S(1)} %reshape.385), channel_id=1, replica_groups=mesh['grid_0'=8,'grid_1'=4,'band_0'=8,'band_1'=2] {'grid_0','grid_1'}, dimensions={0} | all-to-all | bytes 131072 | tf_op jit(solution)/shard_map/all_to_all | solution.py:72
  366.3 3.9 all-to-all-start.7
  370.8 8.4 %all-to-all-done.7 = f32[32,1,512]{2,1,0:T(1,128)S(1)} async-done(((f32[32,1,512]{2,1,0:T(1,128)}), f32[32,1,512]{2,1,0:T(1,128)S(1)}, u32[]{:S(2)}, u32[]{:S(2)}) %all-to-all-start.7) | async-done | bytes 65568 | tf_op jit(solution)/shard_map/all_to_all | solution.py:87
  380.1 1.3 convolution_bitcast_fusion
  381.4 1.3 fusion
  386.9 14.6 %all-reduce.4 = (f32[1,1]{1,0:T(1,128)}, f32[1,1]{1,0:T(1,128)}, f32[1,1]{1,0:T(1,128)}, f32[1,1]{1,0:T(1,128)}, f32[1,1]{1,0:T(1,128)}) all-reduce(f32[1,1]{1,0:T(1,128)} %bitcast.84, f32[1,1]{1,0:T(1,128)} %bitcast.89, f32[1,1]{1,0:T(1,128)} %bitcast.90, ...), channel_id=1, replica_groups=mesh['grid_0'=8,'grid_1'=4,'band_0'=8,'band_1'=2] {'grid_0'}, use_global_device_ids=true, to_apply=%region_85.86 | all-reduce | flops 5 | bytes 40 | tf_op jit(solution)/shard_map/psum | solution.py:17
  401.5 7.5 %all-reduce.8 = (f32[1,1]{1,0:T(1,128)}, f32[1,1]{1,0:T(1,128)}, f32[1,1]{1,0:T(1,128)}, f32[1,1]{1,0:T(1,128)}, f32[1,1]{1,0:T(1,128)}) all-reduce(f32[1,1]{1,0:T(1,128)} %get-tuple-element.44, f32[1,1]{1,0:T(1,128)} %get-tuple-element.45, ...), channel_id=1, replica_groups=mesh['grid_0'=8,'grid_1'=4,'band_0'=8,'band_1'=2] {'grid_1'}, use_global_device_ids=true, to_apply=%region_86.87 | all-reduce | flops 5 | bytes 40 | tf_op jit(solution)/shard_map/psum | solution.py:17
  409.0 13.1 %all-reduce = (f32[1,1]{1,0:T(1,128)}, f32[1,1]{1,0:T(1,128)}, f32[1,1]{1,0:T(1,128)}, f32[1,1]{1,0:T(1,128)}, f32[1,1]{1,0:T(1,128)}) all-reduce(f32[1,1]{1,0:T(1,128)} %get-tuple-element.65, f32[1,1]{1,0:T(1,128)} %get-tuple-element.66, ...), channel_id=1, replica_groups=mesh['grid_0'=8,'grid_1'=4,'band_0'=8,'band_1'=2] {'band_0'}, use_global_device_ids=true, to_apply=%region_87.88 | all-reduce | flops 5 | bytes 40 | tf_op jit(solution)/shard_map/psum | solution.py:17
  422.1 15.2 %all-reduce.12 = (f32[1,1]{1,0:T(1,128)}, f32[1,1]{1,0:T(1,128)}, f32[1,1]{1,0:T(1,128)}, f32[1,1]{1,0:T(1,128)}, f32[1,1]{1,0:T(1,128)}) all-reduce(f32[1,1]{1,0:T(1,128)} %get-tuple-element.23, f32[1,1]{1,0:T(1,128)} %get-tuple-element.24, ...), channel_id=1, replica_groups=mesh['grid_0'=8,'grid_1'=4,'band_0'=8,'band_1'=2] {'band_1'}, use_global_device_ids=true, to_apply=%region_88.89 | all-reduce | flops 5 | bytes 40 | tf_op jit(solution)/shard_map/psum | solution.py:17
  443.5 3.1 pad_maximum_fusion
  (76 shorter events, 28.5 us)
Async XLA Ops:
  0.6 60.8 %copy-start = (f32[1,4,1,4,1024]{4,3,2,1,0:T(4,128)S(1)}, f32[1,4,1,4,1024]{4,3,2,1,0:T(4,128)}, u32[]{:S(2)}) copy-start(f32[1,4,1,4,1024]{4,3,2,1,0:T(4,128)} %param.4) | copy-start | bytes 196612
  64.2 7.8 %copy-start.2 = (f32[32,32,32]{2,1,0:T(8,128)S(1)}, f32[32,32,32]{2,1,0:T(8,128)}, u32[]{:S(2)}) copy-start(f32[32,32,32]{2,1,0:T(8,128)} %param.7) | copy-start | bytes 393220
  65.1 4.9 %copy-start.3 = (s32[3,1]{0,1:T(1,128)S(1)}, s32[3,1]{0,1:T(1,128)}, u32[]{:S(2)}) copy-start(s32[3,1]{0,1:T(1,128)} %param.6) | copy-start | bytes 40
  65.2 13.7 %all-to-all-start = ((f32[32,1,512]{2,1,0:T(1,128)}), f32[32,1,512]{2,1,0:T(1,128)S(1)}, u32[]{:S(2)}, u32[]{:S(2)}) async-start(f32[32,1,512]{2,1,0:T(1,128)} %reshape.373), calls=%async_computation | async-start | bytes 131072 | tf_op jit(solution)/shard_map/all_to_all | solution.py:72
  97.3 0.8 copy-start.1
  177.1 12.8 %all-to-all-start.3 = ((f32[32,1,512]{2,1,0:T(1,128)}), f32[32,1,512]{2,1,0:T(1,128)S(1)}, u32[]{:S(2)}, u32[]{:S(2)}) async-start(f32[32,1,512]{2,1,0:T(1,128)} %reshape.379), calls=%async_computation.3 | async-start | bytes 131072 | tf_op jit(solution)/shard_map/all_to_all | solution.py:87
  272.8 12.8 %all-to-all-start.5 = ((f32[32,1,512]{2,1,0:T(1,128)}), f32[32,1,512]{2,1,0:T(1,128)S(1)}, u32[]{:S(2)}, u32[]{:S(2)}) async-start(f32[32,1,512]{2,1,0:T(1,128)} %reshape.383), calls=%async_computation.5 | async-start | bytes 131072 | tf_op jit(solution)/shard_map/all_to_all | solution.py:87
  366.3 12.8 %all-to-all-start.7 = ((f32[32,1,512]{2,1,0:T(1,128)}), f32[32,1,512]{2,1,0:T(1,128)S(1)}, u32[]{:S(2)}, u32[]{:S(2)}) async-start(f32[32,1,512]{2,1,0:T(1,128)} %reshape.387), calls=%async_computation.7 | async-start | bytes 131072 | tf_op jit(solution)/shard_map/all_to_all | solution.py:87
where the time goes:
time: 448 us; the launch traced here: 447 us
  blocking collectives  307 us (69%)
  between operations  40.5 us (9%)
  waiting for transfers between devices  30.5 us (7%)
  matrix products  24.7 us (6%)
  other arithmetic  17.8 us (4%)
  starting transfers between devices  16.6 us (4%)
  local copies, waits for them, and re-layouts  9.11 us (2%)
    psum x20, blocking collectives, one_axis_at_a_time(): return functools.reduce(lax.psum, axes, x)  256 us
    all_to_all x3, blocking collectives, body(): lax.all_to_all(spread_over_y.reshape(plane_count, grid_size, grid_size, f...  39 us
    all_to_all x3, waiting for transfers between devices, body(): lax.all_to_all(weighted, GRID, split_axis=0, concat_axis=1, tiled=True)  24.8 us
    all_to_all x1, blocking collectives, body(): lax.all_to_all(weighted, GRID, split_axis=0, concat_axis=1, tiled=True)  12.2 us
    all_to_all x3, starting transfers between devices, body(): lax.all_to_all(weighted, GRID, split_axis=0, concat_axis=1, tiled=True)  11.7 us
  transfers between devices with their start and end apart: 4, of which 4 were waited for; matrix products, arithmetic and copies ran while one was open for 0% of the time, Pallas kernels for 0%

commit v1 on v0

--- a/solution.py
+++ b/solution.py
@@ -84,7 +84,10 @@
         scaled = split_view * slab_table[..., None]
         back_x = jnp.einsum("tvwar,xt->xvwar", scaled, cas_grid, precision=precise_mode)
         weighted = back_x.reshape(field_shape)
-        direct_returned = lax.all_to_all(weighted, GRID, split_axis=0, concat_axis=1, tiled=True)
+        direct_returned = jnp.concatenate(
+            lax.all_to_all(jnp.stack(jnp.split(weighted, lax.axis_size(GRID), axis=0)), GRID, 0, 0),
+            axis=1,
+        )
         fields = direct_returned.reshape(plane_count, grid_size, grid_size, atom_count, chain_count)
         over_z = jnp.einsum("pvwar,zw->pvzar", fields, cas_grid, precision=precise_mode)
         over_y = jnp.einsum("pvzar,yv->arpyz", over_z, cas_grid, precision=precise_mode)

time: 448 us -> 450 us (level)
  no operation moved by 1% of the time
where the time goes in v1:
time: 450 us; the launch traced here: 448 us
  blocking collectives  308 us (68%)
  between operations  41.6 us (9%)
  waiting for transfers between devices  30.5 us (7%)
  matrix products  24.7 us (5%)
  other arithmetic  17.8 us (4%)
  starting transfers between devices  16.6 us (4%)
  local copies, waits for them, and re-layouts  9.71 us (2%)
    psum x20, blocking collectives, one_axis_at_a_time(): return functools.reduce(lax.psum, axes, x)  256 us
    all_to_all x3, blocking collectives, body(): lax.all_to_all(spread_over_y.reshape(plane_count, grid_size, grid_size, f...  39.1 us
    all_to_all x3, waiting for transfers between devices, body(): lax.all_to_all(jnp.stack(jnp.split(weighted, lax.axis_size(GRID), axis=0)...  24.8 us
    all_to_all x1, blocking collectives, body(): lax.all_to_all(jnp.stack(jnp.split(weighted, lax.axis_size(GRID), axis=0)...  12.2 us
    all_to_all x3, starting transfers between devices, body(): lax.all_to_all(jnp.stack(jnp.split(weighted, lax.axis_size(GRID), axis=0)...  11.7 us
  transfers between devices with their start and end apart: 4, of which 4 were waited for; matrix products, arithmetic and copies ran while one was open for 0% of the time, Pallas kernels for 0%

profile of v1, /device:TPU:1, one launch (start us, length us, event | category | flops | bytes accessed | tf_op | source)
XLA Modules:
  0.0 448.4 jit_solution(15229270374166463934)
XLA Ops:
  0.6 1.5 multiply_reduce_fusion.20
  2.8 15.8 %psum.652 = f32[1,1]{1,0:T(1,128)} all-reduce(f32[1,1]{1,0:T(1,128)} %bitcast), channel_id=1, replica_groups=mesh['grid_0'=8,'grid_1'=4,'band_0'=8,'band_1'=2] {'grid_0'}, use_global_device_ids=true, to_apply=%region_1.2 | all-reduce | flops 1 | bytes 8 | tf_op jit(solution)/shard_map/psum | solution.py:17
  18.6 9.1 %psum.653 = f32[1,1]{1,0:T(1,128)} all-reduce(f32[1,1]{1,0:T(1,128)} %psum.652), channel_id=1, replica_groups=mesh['grid_0'=8,'grid_1'=4,'band_0'=8,'band_1'=2] {'grid_1'}, use_global_device_ids=true, to_apply=%region_2.3 | all-reduce | flops 1 | bytes 8 | tf_op jit(solution)/shard_map/psum | solution.py:17
  27.7 20.0 %psum.654 = f32[1,1]{1,0:T(1,128)} all-reduce(f32[1,1]{1,0:T(1,128)} %psum.653), channel_id=1, replica_groups=mesh['grid_0'=8,'grid_1'=4,'band_0'=8,'band_1'=2] {'band_0'}, use_global_device_ids=true, to_apply=%region_3.4 | all-reduce | flops 1 | bytes 8 | tf_op jit(solution)/shard_map/psum | solution.py:17
  47.8 12.9 %psum.655 = f32[1,1]{1,0:T(1,128)} all-reduce(f32[1,1]{1,0:T(1,128)} %psum.654), channel_id=1, replica_groups=mesh['grid_0'=8,'grid_1'=4,'band_0'=8,'band_1'=2] {'band_1'}, use_global_device_ids=true, to_apply=%region_4.5 | all-reduce | flops 1 | bytes 8 | tf_op jit(solution)/shard_map/psum | solution.py:17
  62.9 1.3 convolution_bitcast_fusion.10
  65.2 4.8 %all-to-all-start = ((f32[32,1,512]{2,1,0:T(1,128)}), f32[32,1,512]{2,1,0:T(1,128)S(1)}, u32[]{:S(2)}, u32[]{:S(2)}) async-start(f32[32,1,512]{2,1,0:T(1,128)} %reshape.597), calls=%async_computation | async-start | bytes 131072 | tf_op jit(solution)/shard_map/all_to_all | solution.py:72
  73.2 5.6 %all-to-all-done = f32[32,1,512]{2,1,0:T(1,128)S(1)} async-done(((f32[32,1,512]{2,1,0:T(1,128)}), f32[32,1,512]{2,1,0:T(1,128)S(1)}, u32[]{:S(2)}, u32[]{:S(2)}) %all-to-all-start) | async-done | bytes 65568 | tf_op jit(solution)/shard_map/all_to_all | solution.py:72
  82.0 12.2 %all_to_all.56 = f32[32,1,512]{2,1,0:T(1,128)S(1)} all-to-all(f32[32,1,512]{2,1,0:T(1,128)S(1)} %reshape.599), channel_id=1, replica_groups=mesh['grid_0'=8,'grid_1'=4,'band_0'=8,'band_1'=2] {'grid_0','grid_1'}, dimensions={0} | all-to-all | bytes 131072 | tf_op jit(solution)/shard_map/all_to_all | solution.py:88
  95.1 1.3 convolution_bitcast_fusion.9
  96.4 1.3 fusion.3
  102.4 15.4 %all-reduce.7 = (f32[1,1]{1,0:T(1,128)}, f32[1,1]{1,0:T(1,128)}, f32[1,1]{1,0:T(1,128)}, f32[1,1]{1,0:T(1,128)}, f32[1,1]{1,0:T(1,128)}, /*index=5*/f32[1,1]{1,0:T(1,128)}) all-reduce(f32[1,1]{1,0:T(1,128)} %bitcast.55, f32[1,1]{1,0:T(1,128)} %bitcast.52, ...), channel_id=1, replica_groups=mesh['grid_0'=8,'grid_1'=4,'band_0'=8,'band_1'=2] {'grid_0'}, use_global_device_ids=true, to_apply=%region_11.12 | all-reduce | flops 6 | bytes 48 | tf_op jit(solution)/shard_map/psum | solution.py:17
  117.8 7.8 %all-reduce.11 = (f32[1,1]{1,0:T(1,128)}, f32[1,1]{1,0:T(1,128)}, f32[1,1]{1,0:T(1,128)}, f32[1,1]{1,0:T(1,128)}, f32[1,1]{1,0:T(1,128)}, /*index=5*/f32[1,1]{1,0:T(1,128)}) all-reduce(f32[1,1]{1,0:T(1,128)} %get-tuple-element.59, ...), channel_id=1, replica_groups=mesh['grid_0'=8,'grid_1'=4,'band_0'=8,'band_1'=2] {'grid_1'}, use_global_device_ids=true, to_apply=%region_12.13 | all-reduce | flops 6 | bytes 48 | tf_op jit(solution)/shard_map/psum | solution.py:17
  125.6 11.4 %all-reduce.3 = (f32[1,1]{1,0:T(1,128)}, f32[1,1]{1,0:T(1,128)}, f32[1,1]{1,0:T(1,128)}, f32[1,1]{1,0:T(1,128)}, f32[1,1]{1,0:T(1,128)}, /*index=5*/f32[1,1]{1,0:T(1,128)}) all-reduce(f32[1,1]{1,0:T(1,128)} %get-tuple-element.80, ...), channel_id=1, replica_groups=mesh['grid_0'=8,'grid_1'=4,'band_0'=8,'band_1'=2] {'band_0'}, use_global_device_ids=true, to_apply=%region_13.14 | all-reduce | flops 6 | bytes 48 | tf_op jit(solution)/shard_map/psum | solution.py:17
  137.0 14.4 %all-reduce.15 = (f32[1,1]{1,0:T(1,128)}, f32[1,1]{1,0:T(1,128)}, f32[1,1]{1,0:T(1,128)}, f32[1,1]{1,0:T(1,128)}, f32[1,1]{1,0:T(1,128)}, /*index=5*/f32[1,1]{1,0:T(1,128)}) all-reduce(f32[1,1]{1,0:T(1,128)} %get-tuple-element.38, ...), channel_id=1, replica_groups=mesh['grid_0'=8,'grid_1'=4,'band_0'=8,'band_1'=2] {'band_1'}, use_global_device_ids=true, to_apply=%region_14.15 | all-reduce | flops 6 | bytes 48 | tf_op jit(solution)/shard_map/psum | solution.py:17
  158.8 1.3 convolution_bitcast_fusion.8
  160.1 1.3 convolution_bitcast_fusion.7
  161.8 13.1 %all_to_all.57 = f32[32,1,512]{2,1,0:T(1,128)S(1)} all-to-all(f32[32,1,512]{2,1,0:T(1,128)S(1)} %reshape.601), channel_id=1, replica_groups=mesh['grid_0'=8,'grid_1'=4,'band_0'=8,'band_1'=2] {'grid_0','grid_1'}, dimensions={0} | all-to-all | bytes 131072 | tf_op jit(solution)/shard_map/all_to_all | solution.py:72
  178.1 4.0 all-to-all-start.3
  182.8 8.2 %all-to-all-done.3 = f32[32,1,512]{2,1,0:T(1,128)S(1)} async-done(((f32[32,1,512]{2,1,0:T(1,128)}), f32[32,1,512]{2,1,0:T(1,128)S(1)}, u32[]{:S(2)}, u32[]{:S(2)}) %all-to-all-start.3) | async-done | bytes 65568 | tf_op jit(solution)/shard_map/all_to_all | solution.py:88
  191.9 1.3 convolution_bitcast_fusion.6
  193.2 1.3 fusion.2
  198.5 14.7 %all-reduce.6 = (f32[1,1]{1,0:T(1,128)}, f32[1,1]{1,0:T(1,128)}, f32[1,1]{1,0:T(1,128)}, f32[1,1]{1,0:T(1,128)}, f32[1,1]{1,0:T(1,128)}) all-reduce(f32[1,1]{1,0:T(1,128)} %bitcast.107, f32[1,1]{1,0:T(1,128)} %bitcast.104, f32[1,1]{1,0:T(1,128)} %bitcast.108, ...), channel_id=1, replica_groups=mesh['grid_0'=8,'grid_1'=4,'band_0'=8,'band_1'=2] {'grid_0'}, use_global_device_ids=true, to_apply=%region_40.41 | all-reduce | flops 5 | bytes 40 | tf_op jit(solution)/shard_map/psum | solution.py:17
  213.2 7.5 %all-reduce.10 = (f32[1,1]{1,0:T(1,128)}, f32[1,1]{1,0:T(1,128)}, f32[1,1]{1,0:T(1,128)}, f32[1,1]{1,0:T(1,128)}, f32[1,1]{1,0:T(1,128)}) all-reduce(f32[1,1]{1,0:T(1,128)} %get-tuple-element.54, f32[1,1]{1,0:T(1,128)} %get-tuple-element.55, ...), channel_id=1, replica_groups=mesh['grid_0'=8,'grid_1'=4,'band_0'=8,'band_1'=2] {'grid_1'}, use_global_device_ids=true, to_apply=%region_41.42 | all-reduce | flops 5 | bytes 40 | tf_op jit(solution)/shard_map/psum | solution.py:17
  220.7 13.1 %all-reduce.2 = (f32[1,1]{1,0:T(1,128)}, f32[1,1]{1,0:T(1,128)}, f32[1,1]{1,0:T(1,128)}, f32[1,1]{1,0:T(1,128)}, f32[1,1]{1,0:T(1,128)}) all-reduce(f32[1,1]{1,0:T(1,128)} %get-tuple-element.75, f32[1,1]{1,0:T(1,128)} %get-tuple-element.76, ...), channel_id=1, replica_groups=mesh['grid_0'=8,'grid_1'=4,'band_0'=8,'band_1'=2] {'band_0'}, use_global_device_ids=true, to_apply=%region_42.43 | all-reduce | flops 5 | bytes 40 | tf_op jit(solution)/shard_map/psum | solution.py:17
  233.7 15.3 %all-reduce.14 = (f32[1,1]{1,0:T(1,128)}, f32[1,1]{1,0:T(1,128)}, f32[1,1]{1,0:T(1,128)}, f32[1,1]{1,0:T(1,128)}, f32[1,1]{1,0:T(1,128)}) all-reduce(f32[1,1]{1,0:T(1,128)} %get-tuple-element.33, f32[1,1]{1,0:T(1,128)} %get-tuple-element.34, ...), channel_id=1, replica_groups=mesh['grid_0'=8,'grid_1'=4,'band_0'=8,'band_1'=2] {'band_1'}, use_global_device_ids=true, to_apply=%region_43.44 | all-reduce | flops 5 | bytes 40 | tf_op jit(solution)/shard_map/psum | solution.py:17
  256.3 1.3 convolution_bitcast_fusion.4
  257.9 13.0 %all_to_all.58 = f32[32,1,512]{2,1,0:T(1,128)S(1)} all-to-all(f32[32,1,512]{2,1,0:T(1,128)S(1)} %reshape.605), channel_id=1, replica_groups=mesh['grid_0'=8,'grid_1'=4,'band_0'=8,'band_1'=2] {'grid_0','grid_1'}, dimensions={0} | all-to-all | bytes 131072 | tf_op jit(solution)/shard_map/all_to_all | solution.py:72
  274.2 3.9 all-to-all-start.5
  278.7 8.3 %all-to-all-done.5 = f32[32,1,512]{2,1,0:T(1,128)S(1)} async-done(((f32[32,1,512]{2,1,0:T(1,128)}), f32[32,1,512]{2,1,0:T(1,128)S(1)}, u32[]{:S(2)}, u32[]{:S(2)}) %all-to-all-start.5) | async-done | bytes 65568 | tf_op jit(solution)/shard_map/all_to_all | solution.py:88
  288.0 1.3 convolution_bitcast_fusion.3
  289.3 1.3 fusion.1
  294.7 14.7 %all-reduce.5 = (f32[1,1]{1,0:T(1,128)}, f32[1,1]{1,0:T(1,128)}, f32[1,1]{1,0:T(1,128)}, f32[1,1]{1,0:T(1,128)}, f32[1,1]{1,0:T(1,128)}) all-reduce(f32[1,1]{1,0:T(1,128)} %bitcast.159, f32[1,1]{1,0:T(1,128)} %bitcast.156, f32[1,1]{1,0:T(1,128)} %bitcast.160, ...), channel_id=1, replica_groups=mesh['grid_0'=8,'grid_1'=4,'band_0'=8,'band_1'=2] {'grid_0'}, use_global_device_ids=true, to_apply=%region_65.66 | all-reduce | flops 5 | bytes 40 | tf_op jit(solution)/shard_map/psum | solution.py:17
  309.4 7.5 %all-reduce.9 = (f32[1,1]{1,0:T(1,128)}, f32[1,1]{1,0:T(1,128)}, f32[1,1]{1,0:T(1,128)}, f32[1,1]{1,0:T(1,128)}, f32[1,1]{1,0:T(1,128)}) all-reduce(f32[1,1]{1,0:T(1,128)} %get-tuple-element.49, f32[1,1]{1,0:T(1,128)} %get-tuple-element.50, ...), channel_id=1, replica_groups=mesh['grid_0'=8,'grid_1'=4,'band_0'=8,'band_1'=2] {'grid_1'}, use_global_device_ids=true, to_apply=%region_66.67 | all-reduce | flops 5 | bytes 40 | tf_op jit(solution)/shard_map/psum | solution.py:17
  316.9 11.4 %all-reduce.1 = (f32[1,1]{1,0:T(1,128)}, f32[1,1]{1,0:T(1,128)}, f32[1,1]{1,0:T(1,128)}, f32[1,1]{1,0:T(1,128)}, f32[1,1]{1,0:T(1,128)}) all-reduce(f32[1,1]{1,0:T(1,128)} %get-tuple-element.70, f32[1,1]{1,0:T(1,128)} %get-tuple-element.71, ...), channel_id=1, replica_groups=mesh['grid_0'=8,'grid_1'=4,'band_0'=8,'band_1'=2] {'band_0'}, use_global_device_ids=true, to_apply=%region_67.68 | all-reduce | flops 5 | bytes 40 | tf_op jit(solution)/shard_map/psum | solution.py:17
  328.3 15.0 %all-reduce.13 = (f32[1,1]{1,0:T(1,128)}, f32[1,1]{1,0:T(1,128)}, f32[1,1]{1,0:T(1,128)}, f32[1,1]{1,0:T(1,128)}, f32[1,1]{1,0:T(1,128)}) all-reduce(f32[1,1]{1,0:T(1,128)} %get-tuple-element.28, f32[1,1]{1,0:T(1,128)} %get-tuple-element.29, ...), channel_id=1, replica_groups=mesh['grid_0'=8,'grid_1'=4,'band_0'=8,'band_1'=2] {'band_1'}, use_global_device_ids=true, to_apply=%region_68.69 | all-reduce | flops 5 | bytes 40 | tf_op jit(solution)/shard_map/psum | solution.py:17
  349.0 1.3 convolution_bitcast_fusion.2
  350.3 1.3 convolution_bitcast_fusion.1
  352.0 13.0 %all_to_all.59 = f32[32,1,512]{2,1,0:T(1,128)S(1)} all-to-all(f32[32,1,512]{2,1,0:T(1,128)S(1)} %reshape.609), channel_id=1, replica_groups=mesh['grid_0'=8,'grid_1'=4,'band_0'=8,'band_1'=2] {'grid_0','grid_1'}, dimensions={0} | all-to-all | bytes 131072 | tf_op jit(solution)/shard_map/all_to_all | solution.py:72
  368.2 3.9 all-to-all-start.7
  372.6 8.4 %all-to-all-done.7 = f32[32,1,512]{2,1,0:T(1,128)S(1)} async-done(((f32[32,1,512]{2,1,0:T(1,128)}), f32[32,1,512]{2,1,0:T(1,128)S(1)}, u32[]{:S(2)}, u32[]{:S(2)}) %all-to-all-start.7) | async-done | bytes 65568 | tf_op jit(solution)/shard_map/all_to_all | solution.py:88
  382.0 1.3 convolution_bitcast_fusion
  383.3 1.3 fusion
  388.8 14.6 %all-reduce.4 = (f32[1,1]{1,0:T(1,128)}, f32[1,1]{1,0:T(1,128)}, f32[1,1]{1,0:T(1,128)}, f32[1,1]{1,0:T(1,128)}, f32[1,1]{1,0:T(1,128)}) all-reduce(f32[1,1]{1,0:T(1,128)} %bitcast.208, f32[1,1]{1,0:T(1,128)} %bitcast.213, f32[1,1]{1,0:T(1,128)} %bitcast.214, ...), channel_id=1, replica_groups=mesh['grid_0'=8,'grid_1'=4,'band_0'=8,'band_1'=2] {'grid_0'}, use_global_device_ids=true, to_apply=%region_85.86 | all-reduce | flops 5 | bytes 40 | tf_op jit(solution)/shard_map/psum | solution.py:17
  403.4 7.5 %all-reduce.8 = (f32[1,1]{1,0:T(1,128)}, f32[1,1]{1,0:T(1,128)}, f32[1,1]{1,0:T(1,128)}, f32[1,1]{1,0:T(1,128)}, f32[1,1]{1,0:T(1,128)}) all-reduce(f32[1,1]{1,0:T(1,128)} %get-tuple-element.44, f32[1,1]{1,0:T(1,128)} %get-tuple-element.45, ...), channel_id=1, replica_groups=mesh['grid_0'=8,'grid_1'=4,'band_0'=8,'band_1'=2] {'grid_1'}, use_global_device_ids=true, to_apply=%region_86.87 | all-reduce | flops 5 | bytes 40 | tf_op jit(solution)/shard_map/psum | solution.py:17
  410.9 13.1 %all-reduce = (f32[1,1]{1,0:T(1,128)}, f32[1,1]{1,0:T(1,128)}, f32[1,1]{1,0:T(1,128)}, f32[1,1]{1,0:T(1,128)}, f32[1,1]{1,0:T(1,128)}) all-reduce(f32[1,1]{1,0:T(1,128)} %get-tuple-element.65, f32[1,1]{1,0:T(1,128)} %get-tuple-element.66, ...), channel_id=1, replica_groups=mesh['grid_0'=8,'grid_1'=4,'band_0'=8,'band_1'=2] {'band_0'}, use_global_device_ids=true, to_apply=%region_87.88 | all-reduce | flops 5 | bytes 40 | tf_op jit(solution)/shard_map/psum | solution.py:17
  424.0 15.2 %all-reduce.12 = (f32[1,1]{1,0:T(1,128)}, f32[1,1]{1,0:T(1,128)}, f32[1,1]{1,0:T(1,128)}, f32[1,1]{1,0:T(1,128)}, f32[1,1]{1,0:T(1,128)}) all-reduce(f32[1,1]{1,0:T(1,128)} %get-tuple-element.23, f32[1,1]{1,0:T(1,128)} %get-tuple-element.24, ...), channel_id=1, replica_groups=mesh['grid_0'=8,'grid_1'=4,'band_0'=8,'band_1'=2] {'band_1'}, use_global_device_ids=true, to_apply=%region_88.89 | all-reduce | flops 5 | bytes 40 | tf_op jit(solution)/shard_map/psum | solution.py:17
  445.4 3.1 pad_maximum_fusion
  (212 shorter events, 29.1 us)
Async XLA Ops:
  0.6 60.8 %copy-start = (f32[1,4,1,4,1024]{4,3,2,1,0:T(4,128)S(1)}, f32[1,4,1,4,1024]{4,3,2,1,0:T(4,128)}, u32[]{:S(2)}) copy-start(f32[1,4,1,4,1024]{4,3,2,1,0:T(4,128)} %param.4) | copy-start | bytes 196612
  64.2 7.8 %copy-start.2 = (f32[32,32,32]{2,1,0:T(8,128)S(1)}, f32[32,32,32]{2,1,0:T(8,128)}, u32[]{:S(2)}) copy-start(f32[32,32,32]{2,1,0:T(8,128)} %param.7) | copy-start | bytes 393220
  65.1 4.9 %copy-start.3 = (s32[3,1]{0,1:T(1,128)S(1)}, s32[3,1]{0,1:T(1,128)}, u32[]{:S(2)}) copy-start(s32[3,1]{0,1:T(1,128)} %param.6) | copy-start | bytes 40
  65.2 13.7 %all-to-all-start = ((f32[32,1,512]{2,1,0:T(1,128)}), f32[32,1,512]{2,1,0:T(1,128)S(1)}, u32[]{:S(2)}, u32[]{:S(2)}) async-start(f32[32,1,512]{2,1,0:T(1,128)} %reshape.597), calls=%async_computation | async-start | bytes 131072 | tf_op jit(solution)/shard_map/all_to_all | solution.py:72
  97.8 0.8 copy-start.1
  178.1 12.8 %all-to-all-start.3 = ((f32[32,1,512]{2,1,0:T(1,128)}), f32[32,1,512]{2,1,0:T(1,128)S(1)}, u32[]{:S(2)}, u32[]{:S(2)}) async-start(f32[32,1,512]{2,1,0:T(1,128)} %reshape.603), calls=%async_computation.3 | async-start | bytes 131072 | tf_op jit(solution)/shard_map/all_to_all | solution.py:88
  274.2 12.8 %all-to-all-start.5 = ((f32[32,1,512]{2,1,0:T(1,128)}), f32[32,1,512]{2,1,0:T(1,128)S(1)}, u32[]{:S(2)}, u32[]{:S(2)}) async-start(f32[32,1,512]{2,1,0:T(1,128)} %reshape.607), calls=%async_computation.5 | async-start | bytes 131072 | tf_op jit(solution)/shard_map/all_to_all | solution.py:88
  368.2 12.8 %all-to-all-start.7 = ((f32[32,1,512]{2,1,0:T(1,128)}), f32[32,1,512]{2,1,0:T(1,128)S(1)}, u32[]{:S(2)}, u32[]{:S(2)}) async-start(f32[32,1,512]{2,1,0:T(1,128)} %reshape.611), calls=%async_computation.7 | async-start | bytes 131072 | tf_op jit(solution)/shard_map/all_to_all | solution.py:88
